TPU v7x, 128 devices: a whole 4x4x4 slice. The times are simulated.
128 devices in a mesh: pa: 128 (over z, y, x, core).
Axes of the slice: x: 4, y: 4, z: 4, core: 2. Of those that a mesh axis runs over, the one named last changes fastest.
Arguments:
- signal_real: float32 [67108864], P('pa'), may hold values from -6 to 6
- signal_imag: float32 [67108864], P('pa'), may hold values from -6 to 6
Outputs:
- spectrum_real: float32 [67108864], P('pa')
- spectrum_imag: float32 [67108864], P('pa')
All inputs are finite; a program needn't handle non-finite values.
Results may differ from a plain program's by a relative error of at most 0.0003.
Values sent between devices are 32-bit elements.
A program may use at most 128 MiB of HBM per device.

v0:
```python
import math

import jax
import jax.numpy as jnp
from jax import lax
from jax.experimental import pallas as pl
from jax.experimental.pallas import tpu as pltpu
from jax.sharding import PartitionSpec as P

MESH = pl.DeviceIdType.MESH
F32 = jnp.float32
BF16 = jnp.bfloat16
ROOT_HALF = math.sqrt(0.5)
ORDERS = ("zxy", "xyz", "yzx", "zxy", "xyz", "yzx", "zxy", "xyz")


def device(z, y, x, c):
    return ((z * 4 + y) * 4 + x) * 2 + c


def unit_root(phase, bits):
    phase = phase & ((1 << bits) - 1)
    quarter = (phase + (1 << (bits - 3))) >> (bits - 2)
    angle = (phase - (quarter << (bits - 2))).astype(F32) * (2.0 * math.pi / (1 << bits))
    square = angle * angle
    sine = angle * (1.0 + square * (-1 / 6 + square * (1 / 120 + square * (-1 / 5040 + square * (1 / 362880)))))
    cosine = 1.0 + square * (-1 / 2 + square * (1 / 24 + square * (-1 / 720 + square * (1 / 40320))))
    odd = (quarter & 1) == 1
    real = jnp.where(odd, sine, cosine)
    imag = jnp.where(odd, cosine, sine)
    real = jnp.where(((quarter + 1) & 2) == 2, -real, real)
    imag = jnp.where((quarter & 2) == 2, imag, -imag)
    return real, imag


def times(value, factor):
    (a, b), (c, d) = value, factor
    return a * c - b * d, a * d + b * c


def plus(a, b):
    return a[0] + b[0], a[1] + b[1]


def minus(a, b):
    return a[0] - b[0], a[1] - b[1]


def dft4(v):
    s, d = plus(v[0], v[2]), minus(v[0], v[2])
    t, u = plus(v[1], v[3]), minus(v[1], v[3])
    return [plus(s, t), (d[0] + u[1], d[1] - u[0]), minus(s, t), (d[0] - u[1], d[1] + u[0])]


def dft8(v):
    even, odd = dft4(v[0::2]), dft4(v[1::2])
    turned = [
        odd[0],
        ((odd[1][0] + odd[1][1]) * ROOT_HALF, (odd[1][1] - odd[1][0]) * ROOT_HALF),
        (odd[2][1], -odd[2][0]),
        ((odd[3][1] - odd[3][0]) * ROOT_HALF, (odd[3][0] + odd[3][1]) * -ROOT_HALF),
    ]
    return [plus(e, t) for e, t in zip(even, turned)] + [minus(e, t) for e, t in zip(even, turned)]


def split(value):
    high = value.astype(BF16)
    return high, (value - high.astype(F32)).astype(BF16)


def kernel(
    re_hbm, im_hbm, out_re, out_im,
    b1, b2, b3, b4, p0, p1, p2, p3, turn, out, z_hi, z_lo, g_hi, g_lo, h_hi, h_lo, lanes,
    own_sem, send_sem, recv_sem, last_sem, out_sem,
):
    me = lax.axis_index("pa")
    z, y, x, c = me // 32, (me // 8) % 4, (me // 2) % 4, me % 2
    inputs, outputs = (re_hbm, im_hbm), (out_re, out_im)

    barrier = pltpu.get_barrier_semaphore()
    peers = [device(z, (y + d) % 4, x, c) for d in (1, 2, 3)]
    peers += [device(z, y, (x + d) % 4, (c + t) % 2) for d in range(4) for t in range(2) if d + t]
    peers += [device((z + d) % 4, y, x, (c + t) % 2) for d in (1, 2, 3) for t in range(2)]
    for peer in peers:
        pl.semaphore_signal(barrier, inc=1, device_id=(peer,), device_id_type=MESH)
    pl.semaphore_wait(barrier, len(peers))

    def send(src, dst, stage, sem, peer):
        pltpu.make_async_remote_copy(
            src_ref=src, dst_ref=dst, send_sem=send_sem.at[stage], recv_sem=sem, device_id=(peer,), device_id_type=MESH
        ).start()

    def landed(ref, sem):
        pltpu.make_async_remote_copy(
            src_ref=ref, dst_ref=ref, send_sem=sem, recv_sem=sem, device_id=(me,), device_id_type=MESH
        ).wait_recv()

    for q in range(4):
        for part in range(2):

            @pl.loop(0, 8)
            def _(i):
                for d in (1, 3, 2):
                    to = (z + d) % 4
                    send(
                        inputs[part].at[to, :, i * 4 + q, 0],
                        b1.at[q, part, z, i],
                        0, recv_sem.at[0, q], device(to, y, x, c),
                    )
                pltpu.make_async_copy(
                    inputs[part].at[z, :, i * 4 + q, 0], b1.at[q, part, z, i], own_sem.at[q]
                ).start()

    s = z * 32 + c * 16 + x * 4 + y
    rows = lax.broadcasted_iota(jnp.int32, (128, 128), 0)
    cols = lax.broadcasted_iota(jnp.int32, (128, 128), 1)

    def matrix(phase, bits, scale, high, low):
        real, imag = unit_root(phase, bits)
        real, imag = real * scale, imag * scale
        for r, k, block in ((0, 0, real), (0, 1, -imag), (1, 0, imag), (1, 1, real)):
            hi, lo = split(block)
            high[r * 128 : (r + 1) * 128, k * 128 : (k + 1) * 128] = hi
            low[r * 128 : (r + 1) * 128, k * 128 : (k + 1) * 128] = lo

    matrix((rows * 128 + s) * cols, 14, 1.0, g_hi, g_lo)
    target = (rows & 96) + (rows & 3) * 8 + ((rows >> 2) & 3) * 2 + ((rows >> 4) & 1)
    matrix(target * cols, 7, 1.0 / 8192.0, h_hi, h_lo)
    lane_rows = lax.broadcasted_iota(jnp.int32, (32, 128), 0)
    lane_cols = lax.broadcasted_iota(jnp.int32, (32, 128), 1)
    lanes[0], lanes[1] = unit_root(lane_rows * lane_cols, 12)

    @pl.loop(0, 32)
    def _(f):
        real, imag = unit_root((rows * 128 + s) * (cols + f * 128), 26)
        turn[0, f] = real
        turn[1, f] = imag

    def scalar_root(phase, bits):
        return unit_root(jnp.full((8, 128), 1, jnp.int32) * phase, bits)

    turn_y = [scalar_root(k * y, 4) for k in range(4)]
    turn_x = [scalar_root((4 * k + y) * (2 * x + c), 7) for k in range(4)]

    def four(buf, q, factors):
        @pl.loop(0, 8)
        def _(i):
            v = [tuple(buf[q, p, k, i].reshape(4, 8, 128) for p in range(2)) for k in range(4)]
            v = [times(o, (w[0][None], w[1][None])) for o, w in zip(dft4(v), factors)]
            for k in range(4):
                for p in range(2):
                    buf[q, p, k, i] = v[k][p].reshape(32, 128)

    def step_z(q):
        landed(b1.at[q, :, pl.ds(0, 3)], recv_sem.at[0, q])
        pltpu.make_async_copy(b1.at[q, :, 0], b1.at[q, :, 0], own_sem.at[q]).wait()
        four(b1, q, turn_y)
        for d in (1, 3, 2):
            to = (y + d) % 4
            send(b1.at[q, :, to], b2.at[q, :, y], 1, recv_sem.at[1, q], device(z, to, x, c))
        for p in range(2):
            b2[q, p, y] = b1[q, p, y]

    def step_y(q):
        landed(b2.at[q, :, pl.ds(0, 3)], recv_sem.at[1, q])
        four(b2, q, turn_x)
        for d, t in ((1, 0), (3, 0), (2, 0), (1, 1), (3, 1), (2, 1), (0, 1)):
            tx, tc = (x + d) % 4, (c + t) % 2
            send(
                b2.at[q, :, tx, :, pl.ds(pl.multiple_of(tc * 16, 16), 16)],
                b3.at[q, :, x * 2 + c],
                2, recv_sem.at[2, q], device(z, y, tx, tc),
            )
        for p in range(2):
            b3[q, p, x * 2 + c] = b2[q, p, x, :, pl.ds(pl.multiple_of(c * 16, 16), 16)]

    def step_x(q):
        landed(b3.at[q, :, pl.ds(0, 7)], recv_sem.at[2, q])

        @pl.loop(0, 8)
        def _(i):
            v = dft8([(b3[q, 0, k, i], b3[q, 1, k, i]) for k in range(8)])
            for k in range(8):
                b3[q, 0, k, i] = v[k][0]
                b3[q, 1, k, i] = v[k][1]

        for d, t in ((1, 0), (3, 0), (2, 0), (1, 1), (3, 1), (2, 1), (0, 1)):
            tz, tc = (z + d) % 4, (c + t) % 2
            send(
                b3.at[q, :, tz * 2 + tc],
                b4.at[q, :, :, z * 2 + c],
                3, recv_sem.at[3, q], device(tz, y, x, tc),
            )
        for p in range(2):
            b4[q, p, :, z * 2 + c] = b3[q, p, z * 2 + c]

    def step_local(q):
        landed(b4.at[q, :, :, pl.ds(0, 7)], recv_sem.at[3, q])

        @pl.loop(0, 4)
        def _(pair):
            block = jnp.concatenate(
                [
                    jnp.concatenate([b4[q, p, pair * 2 + t].reshape(128, 128) for t in range(2)], axis=1)
                    for p in range(2)
                ],
                axis=0,
            )
            hi, lo = split(block)
            result = jnp.dot(g_hi[...], hi, preferred_element_type=F32)
            result += jnp.dot(g_hi[...], lo, preferred_element_type=F32)
            result += jnp.dot(g_lo[...], hi, preferred_element_type=F32)
            for t in range(2):
                f = (pair * 2 + t) * 4 + q
                value = (result[:128, t * 128 : t * 128 + 128], result[128:, t * 128 : t * 128 + 128])
                value = times(value, (turn[0, f], turn[1, f]))
                for p in range(2):
                    b4[q, p, pair * 2 + t] = value[p].reshape(8, 16, 128)

        @pl.loop(0, 8)
        def _(g):
            v = dft8([(b4[q, 0, i, g], b4[q, 1, i, g]) for i in range(8)])
            for i in range(8):
                b4[q, 0, i, g] = v[i][0]
                b4[q, 1, i, g] = v[i][1]

    def finish(j):
        roots = [
            (math.cos(-2 * math.pi * q * j / 32), math.sin(-2 * math.pi * q * j / 32)) for q in range(4)
        ]

        @pl.loop(0, 8)
        def _(g):
            v = [(b4[q, 0, j, g], b4[q, 1, j, g]) for q in range(4)]
            if j:
                v = [v[0]] + [times(v[q], roots[q]) for q in range(1, 4)]
            v = dft4(v)
            where = pl.ds(pl.multiple_of(g * 16, 16), 16)
            for m in range(4):
                row = j + 8 * m
                w = times(v[m], (lanes[0, row : row + 1], lanes[1, row : row + 1]))
                for p in range(2):
                    hi, lo = split(w[p])
                    z_hi[m, where, p * 128 : (p + 1) * 128] = hi
                    z_lo[m, where, p * 128 : (p + 1) * 128] = lo

        flat = p0.at[j].reshape(1024, 128)
        dims = (((1,), (1,)), ((), ()))
        for pair in range(2):
            hi = z_hi[pair * 2 : pair * 2 + 2].reshape(256, 256)
            lo = z_lo[pair * 2 : pair * 2 + 2].reshape(256, 256)
            result = lax.dot_general(h_hi[...], hi, dims, preferred_element_type=F32)
            result += lax.dot_general(h_hi[...], lo, dims, preferred_element_type=F32)
            result += lax.dot_general(h_lo[...], hi, dims, preferred_element_type=F32)
            for p in range(2):
                for t in range(2):
                    flat[pl.ds(p * 4 + pair * 2 + t, 128, stride=8), :] = result[
                        p * 128 : p * 128 + 128, t * 128 : t * 128 + 128
                    ]

    buffers = (p0, p1, p2, p3)

    def leave(j, stage):
        src, dst, sem = buffers[stage].at[j], buffers[stage + 1].at[j], last_sem.at[stage, j]
        axis = ORDERS[j][stage]
        if axis == "z":
            for d in (1, 3, 2):
                to = (z + d) % 4
                send(src.at[to], dst.at[z], 4 + stage, sem, device(to, y, x, c))
            dst[z] = src[z]
        elif axis == "y":
            for d in (1, 3, 2):
                to = (y + d) % 4
                send(src.at[:, :, :, to], dst.at[:, :, :, y], 4 + stage, sem, device(z, to, x, c))
            dst[:, :, :, y] = src[:, :, :, y]
        else:
            for d, t in ((1, 0), (3, 0), (2, 0), (1, 1), (3, 1), (2, 1), (0, 1)):
                tx, tc = (x + d) % 4, (c + t) % 2
                send(src.at[:, tc, tx], dst.at[:, c, x], 4 + stage, sem, device(z, y, tx, tc))
            dst[:, c, x] = src[:, c, x]

    def arrive(j, stage):
        dst, sem = buffers[stage + 1].at[j], last_sem.at[stage, j]
        axis = ORDERS[j][stage]
        if axis == "z":
            landed(dst.at[pl.ds(0, 3)], sem)
        elif axis == "y":
            landed(dst.at[:, :, :, pl.ds(0, 3)], sem)
        else:
            flat = buffers[stage + 1].at[j].reshape(128, 8, 128)
            landed(flat.at[pl.ds(0, 112)], sem)

    def write(j):
        flat = p3.at[j].reshape(1024, 128)
        for p in range(2):
            for m in range(4):
                row = (j + 8 * m) * 128
                out[p, row : row + 128] = flat[pl.ds(p * 4 + m, 128, stride=8), :].T
                pltpu.make_async_copy(
                    out.at[p, pl.ds(row, 128)], outputs[p].at[pl.ds(row, 128)], out_sem
                ).start()

    step_z(0)
    step_z(1)
    step_y(0)
    step_z(2)
    step_y(1)
    step_x(0)
    step_z(3)
    step_y(2)
    step_x(1)
    step_y(3)
    step_x(2)
    step_local(0)
    step_x(3)
    step_local(1)
    step_local(2)
    step_local(3)

    for j in range(8):
        finish(j)
        leave(j, 0)
    for j, stage in (
        (0, 0), (1, 0), (2, 0), (3, 0), (4, 0), (5, 0), (6, 0), (7, 0), (1, 1), (0, 1), (2, 1), (4, 1),
        (3, 1), (5, 1), (7, 1), (6, 1), (1, 2), (0, 2), (2, 2), (4, 2), (3, 2), (5, 2), (7, 2), (6, 2),
    ):
        arrive(j, stage)
        if stage < 2:
            leave(j, stage + 1)
        else:
            write(j)

    for p in range(2):
        pltpu.make_async_copy(out.at[p], outputs[p], out_sem).wait()

    def sent(ref, stage):
        pltpu.make_async_remote_copy(
            src_ref=ref, dst_ref=ref, send_sem=send_sem.at[stage], recv_sem=send_sem.at[stage],
            device_id=(me,), device_id_type=MESH,
        ).wait_send()

    sent(b1.at[pl.ds(0, 3)], 0)
    sent(b2.at[pl.ds(0, 3)], 1)
    sent(b3.at[:, :, pl.ds(0, 7)], 2)
    sent(b3.at[:, :, pl.ds(0, 7)], 3)
    for stage in range(3):
        eighths = sum(7 if order[stage] == "x" else 6 for order in ORDERS)
        sent(p0.reshape(64, 128, 128).at[pl.ds(0, eighths)], 4 + stage)


def body(signal_real, signal_imag):
    shape = (4, 32, 32, 1, 128)
    block = (8, 4, 2, 4, 4, 8, 128)
    out_re, out_im = pl.pallas_call(
        kernel,
        out_shape=[jax.ShapeDtypeStruct((4096, 128), F32)] * 2,
        in_specs=[pl.BlockSpec(memory_space=pl.ANY)] * 2,
        out_specs=[pl.BlockSpec(memory_space=pl.ANY)] * 2,
        scratch_shapes=[
            pltpu.VMEM((4, 2, 4, 8, 32, 128), F32),
            pltpu.VMEM((4, 2, 4, 8, 32, 128), F32),
            pltpu.VMEM((4, 2, 8, 8, 16, 128), F32),
            pltpu.VMEM((4, 2, 8, 8, 16, 128), F32),
            pltpu.VMEM(block, F32),
            pltpu.VMEM(block, F32),
            pltpu.VMEM(block, F32),
            pltpu.VMEM(block, F32),
            pltpu.VMEM((2, 32, 128, 128), F32),
            pltpu.VMEM((2, 4096, 128), F32),
            pltpu.VMEM((4, 128, 256), BF16),
            pltpu.VMEM((4, 128, 256), BF16),
            pltpu.VMEM((256, 256), BF16),
            pltpu.VMEM((256, 256), BF16),
            pltpu.VMEM((256, 256), BF16),
            pltpu.VMEM((256, 256), BF16),
            pltpu.VMEM((2, 32, 128), F32),
            pltpu.SemaphoreType.DMA((4,)),
            pltpu.SemaphoreType.DMA((7,)),
            pltpu.SemaphoreType.DMA((4, 4)),
            pltpu.SemaphoreType.DMA((3, 8)),
            pltpu.SemaphoreType.DMA,
        ],
        compiler_params=pltpu.CompilerParams(collective_id=0, has_side_effects=True, vmem_limit_bytes=60 * 2**20),
    )(signal_real.reshape(shape), signal_imag.reshape(shape))
    return out_re.reshape(-1), out_im.reshape(-1)


def solution(mesh):
    return jax.shard_map(
        body, mesh=mesh, in_specs=(P("pa"), P("pa")), out_specs=(P("pa"), P("pa")), check_vma=False
    )
```

profile of v0, /device:TPU:1, one launch (start us, length us, event | category | flops | bytes accessed | tf_op | source)
XLA Modules:
  0.0 158.3 jit_solution(5580942445810023981)
XLA Ops:
  0.6 153.0 %shard_map.41 = (f32[4096,128]{1,0:T(8,128)}, f32[4096,128]{1,0:T(8,128)}) custom-call(f32[4,32,32,1,128]{4,3,2,1,0:T(1,128)} %bitcast.4, f32[4,32,32,1,128]{4,3,2,1,0:T(1,128)} %bitcast.5), custom_call_target="tpu_custom_call" | custom-call | tf_op jit(solution)/shard_map/pallas_call | solution.py:354
  153.6 0.0 copy-start
  153.6 3.2 %copy.6 = f32[524288]{0:T(1024)} copy(f32[524288]{0:T(1024)} %bitcast.7) | data formatting | bytes 4194304
  156.8 0.0 copy-done
  156.8 1.5 copy.7
Async XLA Ops:
  153.6 3.2 %copy-start = (f32[4096,128]{1,0:T(8,128)S(1)}, f32[4096,128]{1,0:T(8,128)}, u32[]{:S(2)}) copy-start(f32[4096,128]{1,0:T(8,128)} %get-tuple-element.5) | copy-start | bytes 6291460
where the time goes:
time: 158 us
  Pallas kernels  153 us (97%)
  local copies, waits for them, and re-layouts  4.65 us (3%)
    pallas_call x1, Pallas kernels, body(): pl.pallas_call(kernel, out_shape=[jax.ShapeDtypeStruct((4096, 128), F32)]...  153 us
    unnamed x4, local copies, waits for them, and re-layouts  4.65 us

commit v1 on v0

--- a/solution.py
+++ b/solution.py
@@ -70,8 +70,8 @@
 
 def kernel(
     re_hbm, im_hbm, out_re, out_im,
-    b1, b2, b3, b4, p0, p1, p2, p3, turn, out, z_hi, z_lo, g_hi, g_lo, h_hi, h_lo, lanes,
-    own_sem, send_sem, recv_sem, last_sem, out_sem,
+    b1, b2, b3, b4, p0, p1, p2, p3, turn, z_hi, z_lo, g_hi, g_lo, h_hi, h_lo, lanes,
+    own_sem, send_sem, recv_sem, last_sem,
 ):
     me = lax.axis_index("pa")
     z, y, x, c = me // 32, (me // 8) % 4, (me // 2) % 4, me % 2
@@ -295,10 +295,7 @@
         for p in range(2):
             for m in range(4):
                 row = (j + 8 * m) * 128
-                out[p, row : row + 128] = flat[pl.ds(p * 4 + m, 128, stride=8), :].T
-                pltpu.make_async_copy(
-                    out.at[p, pl.ds(row, 128)], outputs[p].at[pl.ds(row, 128)], out_sem
-                ).start()
+                outputs[p][row : row + 128] = flat[pl.ds(p * 4 + m, 128, stride=8), :].T
 
     step_z(0)
     step_z(1)
@@ -330,9 +327,6 @@
         else:
             write(j)
 
-    for p in range(2):
-        pltpu.make_async_copy(out.at[p], outputs[p], out_sem).wait()
-
     def sent(ref, stage):
         pltpu.make_async_remote_copy(
             src_ref=ref, dst_ref=ref, send_sem=send_sem.at[stage], recv_sem=send_sem.at[stage],
@@ -348,14 +342,26 @@
         sent(p0.reshape(64, 128, 128).at[pl.ds(0, eighths)], 4 + stage)
 
 
+def store(re_ref, im_ref, out_re, out_im, sems):
+    copies = [
+        pltpu.make_async_copy(src.at[pl.ds(k * 512, 512)], dst.at[pl.ds(k * 512, 512)], sems.at[p, k])
+        for k in range(8)
+        for p, (src, dst) in enumerate(((re_ref, out_re), (im_ref, out_im)))
+    ]
+    for copy in copies:
+        copy.start()
+    for copy in copies:
+        copy.wait()
+
+
 def body(signal_real, signal_imag):
     shape = (4, 32, 32, 1, 128)
     block = (8, 4, 2, 4, 4, 8, 128)
-    out_re, out_im = pl.pallas_call(
+    spectrum = pl.pallas_call(
         kernel,
-        out_shape=[jax.ShapeDtypeStruct((4096, 128), F32)] * 2,
+        out_shape=[pltpu.VMEM((4096, 128), F32)] * 2,
         in_specs=[pl.BlockSpec(memory_space=pl.ANY)] * 2,
-        out_specs=[pl.BlockSpec(memory_space=pl.ANY)] * 2,
+        out_specs=[pl.BlockSpec(memory_space=pltpu.VMEM)] * 2,
         scratch_shapes=[
             pltpu.VMEM((4, 2, 4, 8, 32, 128), F32),
             pltpu.VMEM((4, 2, 4, 8, 32, 128), F32),
@@ -366,7 +372,6 @@
             pltpu.VMEM(block, F32),
             pltpu.VMEM(block, F32),
             pltpu.VMEM((2, 32, 128, 128), F32),
-            pltpu.VMEM((2, 4096, 128), F32),
             pltpu.VMEM((4, 128, 256), BF16),
             pltpu.VMEM((4, 128, 256), BF16),
             pltpu.VMEM((256, 256), BF16),
@@ -378,10 +383,17 @@
             pltpu.SemaphoreType.DMA((7,)),
             pltpu.SemaphoreType.DMA((4, 4)),
             pltpu.SemaphoreType.DMA((3, 8)),
-            pltpu.SemaphoreType.DMA,
         ],
-        compiler_params=pltpu.CompilerParams(collective_id=0, has_side_effects=True, vmem_limit_bytes=60 * 2**20),
+        compiler_params=pltpu.CompilerParams(collective_id=0, has_side_effects=True, vmem_limit_bytes=48 * 2**20),
     )(signal_real.reshape(shape), signal_imag.reshape(shape))
+    out_re, out_im = pl.pallas_call(
+        store,
+        out_shape=[jax.ShapeDtypeStruct((4096, 128), F32)] * 2,
+        in_specs=[pl.BlockSpec(memory_space=pltpu.VMEM)] * 2,
+        out_specs=[pl.BlockSpec(memory_space=pl.ANY)] * 2,
+        scratch_shapes=[pltpu.SemaphoreType.DMA((2, 8))],
+        compiler_params=pltpu.CompilerParams(vmem_limit_bytes=8 * 2**20),
+    )(*spectrum)
     return out_re.reshape(-1), out_im.reshape(-1)
 
 

time: 158 us -> 155 us (0.981)
  local copies, waits for them, and re-layouts: 4.65 us -> 0 us
    unnamed x4 -> x0, local copies, waits for them, and re-layouts: 4.65 us -> none
    pallas_call x1 -> x2, Pallas kernels: 153 us -> 154 us  [the longest x1 152 us: body(): pl.pallas_call(kernel, out_shape=[pltpu.VMEM((4096, 128), F32)] * 2, in_s...]
where the time goes in v1:
time: 155 us
  Pallas kernels  154 us (99%)
    pallas_call x1, Pallas kernels, body(): pl.pallas_call(kernel, out_shape=[pltpu.VMEM((4096, 128), F32)] * 2, in_s...  152 us

profile of v1, /device:TPU:1, one launch (start us, length us, event | category | flops | bytes accessed | tf_op | source)
XLA Modules:
  0.0 155.0 jit_solution(7887810208273766694)
XLA Ops:
  0.6 152.2 %shard_map.41 = (f32[4096,128]{1,0:T(8,128)S(1)}, f32[4096,128]{1,0:T(8,128)S(1)}) custom-call(f32[4,32,32,1,128]{4,3,2,1,0:T(1,128)} %bitcast.4, f32[4,32,32,1,128]{4,3,2,1,0:T(1,128)} %bitcast.5), custom_call_target="tpu_custom_call" | custom-call | tf_op jit(solution)/shard_map/pallas_call | solution.py:360
  152.9 2.1 %shard_map.42 = (f32[4096,128]{1,0:T(8,128)}, f32[4096,128]{1,0:T(8,128)}) custom-call(f32[4096,128]{1,0:T(8,128)S(1)} %get-tuple-element.6.re_ref, f32[4096,128]{1,0:T(8,128)S(1)} %get-tuple-element.7.im_ref), custom_call_target="tpu_custom_call" | custom-call | tf_op jit(solution)/shard_map/pallas_call | solution.py:389

commit v2 on v1

--- a/solution.py
+++ b/solution.py
@@ -11,7 +11,7 @@
 F32 = jnp.float32
 BF16 = jnp.bfloat16
 ROOT_HALF = math.sqrt(0.5)
-ORDERS = ("zxy", "xyz", "yzx", "zxy", "xyz", "yzx", "zxy", "xyz")
+ORDERS = ('yxz', 'zyx', 'xzy', 'zyx', 'xzy', 'xyz', 'yxz', 'zyx')
 
 
 def device(z, y, x, c):
@@ -70,7 +70,7 @@
 
 def kernel(
     re_hbm, im_hbm, out_re, out_im,
-    b1, b2, b3, b4, p0, p1, p2, p3, turn, z_hi, z_lo, g_hi, g_lo, h_hi, h_lo, lanes,
+    b1, b2, b3, b4, p0, p1, p2, p3, turn, z_hi, z_lo, g, h, lanes,
     own_sem, send_sem, recv_sem, last_sem,
 ):
     me = lax.axis_index("pa")
@@ -100,7 +100,7 @@
 
             @pl.loop(0, 8)
             def _(i):
-                for d in (1, 3, 2):
+                for d in (2, 1, 3):
                     to = (z + d) % 4
                     send(
                         inputs[part].at[to, :, i * 4 + q, 0],
@@ -115,17 +115,17 @@
     rows = lax.broadcasted_iota(jnp.int32, (128, 128), 0)
     cols = lax.broadcasted_iota(jnp.int32, (128, 128), 1)
 
-    def matrix(phase, bits, scale, high, low):
+    def matrix(phase, bits, scale, table):
         real, imag = unit_root(phase, bits)
         real, imag = real * scale, imag * scale
         for r, k, block in ((0, 0, real), (0, 1, -imag), (1, 0, imag), (1, 1, real)):
             hi, lo = split(block)
-            high[r * 128 : (r + 1) * 128, k * 128 : (k + 1) * 128] = hi
-            low[r * 128 : (r + 1) * 128, k * 128 : (k + 1) * 128] = lo
-
-    matrix((rows * 128 + s) * cols, 14, 1.0, g_hi, g_lo)
+            table[r * 128 : r * 128 + 128, k * 128 : k * 128 + 128] = hi
+            table[r * 128 + 256 : r * 128 + 384, k * 128 : k * 128 + 128] = lo
+
+    matrix((rows * 128 + s) * cols, 14, 1.0, g)
     target = (rows & 96) + (rows & 3) * 8 + ((rows >> 2) & 3) * 2 + ((rows >> 4) & 1)
-    matrix(target * cols, 7, 1.0 / 8192.0, h_hi, h_lo)
+    matrix(target * cols, 7, 1.0 / 8192.0, h)
     lane_rows = lax.broadcasted_iota(jnp.int32, (32, 128), 0)
     lane_cols = lax.broadcasted_iota(jnp.int32, (32, 128), 1)
     lanes[0], lanes[1] = unit_root(lane_rows * lane_cols, 12)
@@ -155,7 +155,7 @@
         landed(b1.at[q, :, pl.ds(0, 3)], recv_sem.at[0, q])
         pltpu.make_async_copy(b1.at[q, :, 0], b1.at[q, :, 0], own_sem.at[q]).wait()
         four(b1, q, turn_y)
-        for d in (1, 3, 2):
+        for d in (2, 1, 3):
             to = (y + d) % 4
             send(b1.at[q, :, to], b2.at[q, :, y], 1, recv_sem.at[1, q], device(z, to, x, c))
         for p in range(2):
@@ -164,7 +164,7 @@
     def step_y(q):
         landed(b2.at[q, :, pl.ds(0, 3)], recv_sem.at[1, q])
         four(b2, q, turn_x)
-        for d, t in ((1, 0), (3, 0), (2, 0), (1, 1), (3, 1), (2, 1), (0, 1)):
+        for d, t in ((2, 1), (2, 0), (1, 1), (3, 1), (1, 0), (3, 0), (0, 1)):
             tx, tc = (x + d) % 4, (c + t) % 2
             send(
                 b2.at[q, :, tx, :, pl.ds(pl.multiple_of(tc * 16, 16), 16)],
@@ -184,20 +184,24 @@
                 b3[q, 0, k, i] = v[k][0]
                 b3[q, 1, k, i] = v[k][1]
 
-        for d, t in ((1, 0), (3, 0), (2, 0), (1, 1), (3, 1), (2, 1), (0, 1)):
-            tz, tc = (z + d) % 4, (c + t) % 2
+        def leave_x(tz, tc):
             send(
                 b3.at[q, :, tz * 2 + tc],
                 b4.at[q, :, :, z * 2 + c],
                 3, recv_sem.at[3, q], device(tz, y, x, tc),
             )
+
+        leave_x(z, 1 - c)
+        for tc in range(2):
+            for d in (2, 1, 3):
+                leave_x((z + d) % 4, tc)
         for p in range(2):
             b4[q, p, :, z * 2 + c] = b3[q, p, z * 2 + c]
 
     def step_local(q):
         landed(b4.at[q, :, :, pl.ds(0, 7)], recv_sem.at[3, q])
 
-        @pl.loop(0, 4)
+        @pl.loop(0, 4, unroll=True)
         def _(pair):
             block = jnp.concatenate(
                 [
@@ -207,9 +211,8 @@
                 axis=0,
             )
             hi, lo = split(block)
-            result = jnp.dot(g_hi[...], hi, preferred_element_type=F32)
-            result += jnp.dot(g_hi[...], lo, preferred_element_type=F32)
-            result += jnp.dot(g_lo[...], hi, preferred_element_type=F32)
+            both = jnp.dot(g[...], hi, preferred_element_type=F32)
+            result = both[:256] + both[256:] + jnp.dot(g[:256], lo, preferred_element_type=F32)
             for t in range(2):
                 f = (pair * 2 + t) * 4 + q
                 value = (result[:128, t * 128 : t * 128 + 128], result[128:, t * 128 : t * 128 + 128])
@@ -217,7 +220,7 @@
                 for p in range(2):
                     b4[q, p, pair * 2 + t] = value[p].reshape(8, 16, 128)
 
-        @pl.loop(0, 8)
+        @pl.loop(0, 8, unroll=True)
         def _(g):
             v = dft8([(b4[q, 0, i, g], b4[q, 1, i, g]) for i in range(8)])
             for i in range(8):
@@ -229,7 +232,7 @@
             (math.cos(-2 * math.pi * q * j / 32), math.sin(-2 * math.pi * q * j / 32)) for q in range(4)
         ]
 
-        @pl.loop(0, 8)
+        @pl.loop(0, 8, unroll=True)
         def _(g):
             v = [(b4[q, 0, j, g], b4[q, 1, j, g]) for q in range(4)]
             if j:
@@ -249,9 +252,8 @@
         for pair in range(2):
             hi = z_hi[pair * 2 : pair * 2 + 2].reshape(256, 256)
             lo = z_lo[pair * 2 : pair * 2 + 2].reshape(256, 256)
-            result = lax.dot_general(h_hi[...], hi, dims, preferred_element_type=F32)
-            result += lax.dot_general(h_hi[...], lo, dims, preferred_element_type=F32)
-            result += lax.dot_general(h_lo[...], hi, dims, preferred_element_type=F32)
+            both = lax.dot_general(h[...], hi, dims, preferred_element_type=F32)
+            result = both[:256] + both[256:] + lax.dot_general(h[:256], lo, dims, preferred_element_type=F32)
             for p in range(2):
                 for t in range(2):
                     flat[pl.ds(p * 4 + pair * 2 + t, 128, stride=8), :] = result[
@@ -264,17 +266,17 @@
         src, dst, sem = buffers[stage].at[j], buffers[stage + 1].at[j], last_sem.at[stage, j]
         axis = ORDERS[j][stage]
         if axis == "z":
-            for d in (1, 3, 2):
+            for d in (2, 1, 3):
                 to = (z + d) % 4
                 send(src.at[to], dst.at[z], 4 + stage, sem, device(to, y, x, c))
             dst[z] = src[z]
         elif axis == "y":
-            for d in (1, 3, 2):
+            for d in (2, 1, 3):
                 to = (y + d) % 4
                 send(src.at[:, :, :, to], dst.at[:, :, :, y], 4 + stage, sem, device(z, to, x, c))
             dst[:, :, :, y] = src[:, :, :, y]
         else:
-            for d, t in ((1, 0), (3, 0), (2, 0), (1, 1), (3, 1), (2, 1), (0, 1)):
+            for d, t in ((2, 1), (2, 0), (1, 1), (3, 1), (1, 0), (3, 0), (0, 1)):
                 tx, tc = (x + d) % 4, (c + t) % 2
                 send(src.at[:, tc, tx], dst.at[:, c, x], 4 + stage, sem, device(z, y, tx, tc))
             dst[:, c, x] = src[:, c, x]
@@ -317,10 +319,7 @@
     for j in range(8):
         finish(j)
         leave(j, 0)
-    for j, stage in (
-        (0, 0), (1, 0), (2, 0), (3, 0), (4, 0), (5, 0), (6, 0), (7, 0), (1, 1), (0, 1), (2, 1), (4, 1),
-        (3, 1), (5, 1), (7, 1), (6, 1), (1, 2), (0, 2), (2, 2), (4, 2), (3, 2), (5, 2), (7, 2), (6, 2),
-    ):
+    for j, stage in ((0, 0), (1, 0), (2, 0), (6, 0), (3, 0), (4, 0), (1, 1), (7, 0), (5, 0), (3, 1), (2, 1), (0, 1), (7, 1), (4, 1), (6, 1), (5, 1), (0, 2), (1, 2), (2, 2), (6, 2), (3, 2), (4, 2), (5, 2), (7, 2)):
         arrive(j, stage)
         if stage < 2:
             leave(j, stage + 1)
@@ -374,10 +373,8 @@
             pltpu.VMEM((2, 32, 128, 128), F32),
             pltpu.VMEM((4, 128, 256), BF16),
             pltpu.VMEM((4, 128, 256), BF16),
-            pltpu.VMEM((256, 256), BF16),
-            pltpu.VMEM((256, 256), BF16),
-            pltpu.VMEM((256, 256), BF16),
-            pltpu.VMEM((256, 256), BF16),
+            pltpu.VMEM((512, 256), BF16),
+            pltpu.VMEM((512, 256), BF16),
             pltpu.VMEM((2, 32, 128), F32),
             pltpu.SemaphoreType.DMA((4,)),
             pltpu.SemaphoreType.DMA((7,)),

time: 155 us -> 151 us (0.974)
  Pallas kernels: 154 us -> 150 us
    pallas_call x1, Pallas kernels: 152 us -> 148 us  [body(): pl.pallas_call(kernel, out_shape=[pltpu.VMEM((4096, 128), F32)] * 2, in_s...]
where the time goes in v2:
time: 151 us
  Pallas kernels  150 us (99%)
    pallas_call x1, Pallas kernels, body(): pl.pallas_call(kernel, out_shape=[pltpu.VMEM((4096, 128), F32)] * 2, in_s...  148 us

profile of v2, /device:TPU:1, one launch (start us, length us, event | category | flops | bytes accessed | tf_op | source)
XLA Modules:
  0.0 151.0 jit_solution(2288574912523854550)
XLA Ops:
  0.6 148.2 %shard_map.41 = (f32[4096,128]{1,0:T(8,128)S(1)}, f32[4096,128]{1,0:T(8,128)S(1)}) custom-call(f32[4,32,32,1,128]{4,3,2,1,0:T(1,128)} %bitcast.4, f32[4,32,32,1,128]{4,3,2,1,0:T(1,128)} %bitcast.5), custom_call_target="tpu_custom_call" | custom-call | tf_op jit(solution)/shard_map/pallas_call | solution.py:359
  148.9 2.1 %shard_map.42 = (f32[4096,128]{1,0:T(8,128)}, f32[4096,128]{1,0:T(8,128)}) custom-call(f32[4096,128]{1,0:T(8,128)S(1)} %get-tuple-element.6.re_ref, f32[4096,128]{1,0:T(8,128)S(1)} %get-tuple-element.7.im_ref), custom_call_target="tpu_custom_call" | custom-call | tf_op jit(solution)/shard_map/pallas_call | solution.py:386

commit v3 on v2

--- a/solution.py
+++ b/solution.py
@@ -70,19 +70,25 @@
 
 def kernel(
     re_hbm, im_hbm, out_re, out_im,
-    b1, b2, b3, b4, p0, p1, p2, p3, turn, z_hi, z_lo, g, h, lanes,
-    own_sem, send_sem, recv_sem, last_sem,
+    b1, b2, b3, b4, p0, p1, p2, p3, turn, z_hi, z_lo, g, h, lanes, first,
+    own_sem, first_sem, send_sem, recv_sem, last_sem,
 ):
     me = lax.axis_index("pa")
     z, y, x, c = me // 32, (me // 8) % 4, (me // 2) % 4, me % 2
     inputs, outputs = (re_hbm, im_hbm), (out_re, out_im)
 
     barrier = pltpu.get_barrier_semaphore()
-    peers = [device(z, (y + d) % 4, x, c) for d in (1, 2, 3)]
-    peers += [device(z, y, (x + d) % 4, (c + t) % 2) for d in range(4) for t in range(2) if d + t]
-    peers += [device((z + d) % 4, y, x, (c + t) % 2) for d in (1, 2, 3) for t in range(2)]
+    peers = [device((z + d) % 4, y, x, (c + t) % 2) for t in range(2) for d in (2, 1, 3)]
+    peers += [device(z, y, (x + d) % 4, (c + t) % 2) for d in (2, 1, 3, 0) for t in range(2) if d + t]
+    peers += [device(z, (y + d) % 4, x, c) for d in (2, 1, 3)]
     for peer in peers:
         pl.semaphore_signal(barrier, inc=1, device_id=(peer,), device_id_type=MESH)
+    for part in range(2):
+
+        @pl.loop(0, 8)
+        def _(i):
+            pltpu.make_async_copy(inputs[part].at[:, :, i * 4, 0], first.at[part, i], first_sem.at[part]).start()
+
     pl.semaphore_wait(barrier, len(peers))
 
     def send(src, dst, stage, sem, peer):
@@ -95,7 +101,12 @@
             src_ref=ref, dst_ref=ref, send_sem=sem, recv_sem=sem, device_id=(me,), device_id_type=MESH
         ).wait_recv()
 
-    for q in range(4):
+    for part in range(2):
+        pltpu.make_async_copy(first.at[part], first.at[part], first_sem.at[part]).wait()
+        for d in (2, 1, 3):
+            to = (z + d) % 4
+            send(first.at[part, :, to], b1.at[0, part, z], 0, recv_sem.at[0, 0], device(to, y, x, c))
+    for q in range(1, 4):
         for part in range(2):
 
             @pl.loop(0, 8)
@@ -110,6 +121,8 @@
                 pltpu.make_async_copy(
                     inputs[part].at[z, :, i * 4 + q, 0], b1.at[q, part, z, i], own_sem.at[q]
                 ).start()
+    for part in range(2):
+        b1[0, part, z] = first[part, :, z]
 
     s = z * 32 + c * 16 + x * 4 + y
     rows = lax.broadcasted_iota(jnp.int32, (128, 128), 0)
@@ -153,7 +166,8 @@
 
     def step_z(q):
         landed(b1.at[q, :, pl.ds(0, 3)], recv_sem.at[0, q])
-        pltpu.make_async_copy(b1.at[q, :, 0], b1.at[q, :, 0], own_sem.at[q]).wait()
+        if q:
+            pltpu.make_async_copy(b1.at[q, :, 0], b1.at[q, :, 0], own_sem.at[q]).wait()
         four(b1, q, turn_y)
         for d in (2, 1, 3):
             to = (y + d) % 4
@@ -376,7 +390,9 @@
             pltpu.VMEM((512, 256), BF16),
             pltpu.VMEM((512, 256), BF16),
             pltpu.VMEM((2, 32, 128), F32),
+            pltpu.VMEM((2, 8, 4, 32, 128), F32),
             pltpu.SemaphoreType.DMA((4,)),
+            pltpu.SemaphoreType.DMA((2,)),
             pltpu.SemaphoreType.DMA((7,)),
             pltpu.SemaphoreType.DMA((4, 4)),
             pltpu.SemaphoreType.DMA((3, 8)),

time: 151 us -> 150 us (level)
  no operation moved by 1% of the time
where the time goes in v3:
time: 150 us
  Pallas kernels  149 us (99%)
    pallas_call x1, Pallas kernels, body(): pl.pallas_call(kernel, out_shape=[pltpu.VMEM((4096, 128), F32)] * 2, in_s...  147 us

profile of v3, /device:TPU:1, one launch (start us, length us, event | category | flops | bytes accessed | tf_op | source)
XLA Modules:
  0.0 149.8 jit_solution(6306292269080644705)
XLA Ops:
  0.6 147.1 %shard_map.41 = (f32[4096,128]{1,0:T(8,128)S(1)}, f32[4096,128]{1,0:T(8,128)S(1)}) custom-call(f32[4,32,32,1,128]{4,3,2,1,0:T(1,128)} %bitcast.4, f32[4,32,32,1,128]{4,3,2,1,0:T(1,128)} %bitcast.5), custom_call_target="tpu_custom_call" | custom-call | tf_op jit(solution)/shard_map/pallas_call | solution.py:373
  147.7 2.1 %shard_map.42 = (f32[4096,128]{1,0:T(8,128)}, f32[4096,128]{1,0:T(8,128)}) custom-call(f32[4096,128]{1,0:T(8,128)S(1)} %get-tuple-element.6.re_ref, f32[4096,128]{1,0:T(8,128)S(1)} %get-tuple-element.7.im_ref), custom_call_target="tpu_custom_call" | custom-call | tf_op jit(solution)/shard_map/pallas_call | solution.py:402

commit v4 on v3

--- a/solution.py
+++ b/solution.py
@@ -206,7 +206,7 @@
             )
 
         leave_x(z, 1 - c)
-        for tc in range(2):
+        for tc in (1, 0):
             for d in (2, 1, 3):
                 leave_x((z + d) % 4, tc)
         for p in range(2):

time: 150 us -> 149 us (level)
  no operation moved by 1% of the time
where the time goes in v4:
time: 149 us
  Pallas kernels  148 us (99%)
    pallas_call x1, Pallas kernels, body(): pl.pallas_call(kernel, out_shape=[pltpu.VMEM((4096, 128), F32)] * 2, in_s...  146 us

profile of v4, /device:TPU:1, one launch (start us, length us, event | category | flops | bytes accessed | tf_op | source)
XLA Modules:
  0.0 148.7 jit_solution(10930466983680049854)
XLA Ops:
  0.6 145.9 %shard_map.41 = (f32[4096,128]{1,0:T(8,128)S(1)}, f32[4096,128]{1,0:T(8,128)S(1)}) custom-call(f32[4,32,32,1,128]{4,3,2,1,0:T(1,128)} %bitcast.4, f32[4,32,32,1,128]{4,3,2,1,0:T(1,128)} %bitcast.5), custom_call_target="tpu_custom_call" | custom-call | tf_op jit(solution)/shard_map/pallas_call | solution.py:373
  146.5 2.1 %shard_map.42 = (f32[4096,128]{1,0:T(8,128)}, f32[4096,128]{1,0:T(8,128)}) custom-call(f32[4096,128]{1,0:T(8,128)S(1)} %get-tuple-element.6.re_ref, f32[4096,128]{1,0:T(8,128)S(1)} %get-tuple-element.7.im_ref), custom_call_target="tpu_custom_call" | custom-call | tf_op jit(solution)/shard_map/pallas_call | solution.py:402

commit v5 on v4

--- a/solution.py
+++ b/solution.py
@@ -290,9 +290,11 @@
                 send(src.at[:, :, :, to], dst.at[:, :, :, y], 4 + stage, sem, device(z, to, x, c))
             dst[:, :, :, y] = src[:, :, :, y]
         else:
-            for d, t in ((2, 1), (2, 0), (1, 1), (3, 1), (1, 0), (3, 0), (0, 1)):
-                tx, tc = (x + d) % 4, (c + t) % 2
-                send(src.at[:, tc, tx], dst.at[:, c, x], 4 + stage, sem, device(z, y, tx, tc))
+            send(src.at[:, 1 - c, x], dst.at[:, c, x], 4 + stage, sem, device(z, y, x, 1 - c))
+            for tc in (1, 0):
+                for d in (2, 1, 3):
+                    tx = (x + d) % 4
+                    send(src.at[:, tc, tx], dst.at[:, c, x], 4 + stage, sem, device(z, y, tx, tc))
             dst[:, c, x] = src[:, c, x]
 
     def arrive(j, stage):

time: 149 us -> 149 us (level)
  no operation moved by 1% of the time
where the time goes in v5:
time: 149 us; the launch traced here: 148 us
  Pallas kernels  147 us (99%)
    pallas_call x1, Pallas kernels, body(): pl.pallas_call(kernel, out_shape=[pltpu.VMEM((4096, 128), F32)] * 2, in_s...  145 us

profile of v5, /device:TPU:1, one launch (start us, length us, event | category | flops | bytes accessed | tf_op | source)
XLA Modules:
  0.0 147.7 jit_solution(17682874904828098946)
XLA Ops:
  0.6 145.0 %shard_map.41 = (f32[4096,128]{1,0:T(8,128)S(1)}, f32[4096,128]{1,0:T(8,128)S(1)}) custom-call(f32[4,32,32,1,128]{4,3,2,1,0:T(1,128)} %bitcast.4, f32[4,32,32,1,128]{4,3,2,1,0:T(1,128)} %bitcast.5), custom_call_target="tpu_custom_call" | custom-call | tf_op jit(solution)/shard_map/pallas_call | solution.py:375
  145.6 2.1 %shard_map.42 = (f32[4096,128]{1,0:T(8,128)}, f32[4096,128]{1,0:T(8,128)}) custom-call(f32[4096,128]{1,0:T(8,128)S(1)} %get-tuple-element.6.re_ref, f32[4096,128]{1,0:T(8,128)S(1)} %get-tuple-element.7.im_ref), custom_call_target="tpu_custom_call" | custom-call | tf_op jit(solution)/shard_map/pallas_call | solution.py:404

commit v6 on v4

--- a/solution.py
+++ b/solution.py
@@ -333,26 +333,30 @@
     for j in range(8):
         finish(j)
         leave(j, 0)
+    def sent(ref, stage):
+        pltpu.make_async_remote_copy(
+            src_ref=ref, dst_ref=ref, send_sem=send_sem.at[stage], recv_sem=send_sem.at[stage],
+            device_id=(me,), device_id_type=MESH,
+        ).wait_send()
+
+    def sent_last(stage):
+        eighths = sum(7 if order[stage] == "x" else 6 for order in ORDERS)
+        sent(p0.reshape(64, 128, 128).at[pl.ds(0, eighths)], 4 + stage)
+
     for j, stage in ((0, 0), (1, 0), (2, 0), (6, 0), (3, 0), (4, 0), (1, 1), (7, 0), (5, 0), (3, 1), (2, 1), (0, 1), (7, 1), (4, 1), (6, 1), (5, 1), (0, 2), (1, 2), (2, 2), (6, 2), (3, 2), (4, 2), (5, 2), (7, 2)):
+        if (j, stage) == (5, 2):
+            sent(b1.at[pl.ds(0, 3)], 0)
+            sent(b2.at[pl.ds(0, 3)], 1)
+            sent(b3.at[:, :, pl.ds(0, 7)], 2)
+            sent(b3.at[:, :, pl.ds(0, 7)], 3)
+            sent_last(0)
+            sent_last(1)
         arrive(j, stage)
         if stage < 2:
             leave(j, stage + 1)
         else:
             write(j)
-
-    def sent(ref, stage):
-        pltpu.make_async_remote_copy(
-            src_ref=ref, dst_ref=ref, send_sem=send_sem.at[stage], recv_sem=send_sem.at[stage],
-            device_id=(me,), device_id_type=MESH,
-        ).wait_send()
-
-    sent(b1.at[pl.ds(0, 3)], 0)
-    sent(b2.at[pl.ds(0, 3)], 1)
-    sent(b3.at[:, :, pl.ds(0, 7)], 2)
-    sent(b3.at[:, :, pl.ds(0, 7)], 3)
-    for stage in range(3):
-        eighths = sum(7 if order[stage] == "x" else 6 for order in ORDERS)
-        sent(p0.reshape(64, 128, 128).at[pl.ds(0, eighths)], 4 + stage)
+    sent_last(2)
 
 
 def store(re_ref, im_ref, out_re, out_im, sems):

time: 149 us -> 149 us (level)
  no operation moved by 1% of the time
where the time goes in v6:
time: 149 us
  Pallas kernels  148 us (99%)
    pallas_call x1, Pallas kernels, body(): pl.pallas_call(kernel, out_shape=[pltpu.VMEM((4096, 128), F32)] * 2, in_s...  146 us

profile of v6, /device:TPU:1, one launch (start us, length us, event | category | flops | bytes accessed | tf_op | source)
XLA Modules:
  0.0 148.7 jit_solution(10571373574758673854)
XLA Ops:
  0.6 145.9 %shard_map.41 = (f32[4096,128]{1,0:T(8,128)S(1)}, f32[4096,128]{1,0:T(8,128)S(1)}) custom-call(f32[4,32,32,1,128]{4,3,2,1,0:T(1,128)} %bitcast.4, f32[4,32,32,1,128]{4,3,2,1,0:T(1,128)} %bitcast.5), custom_call_target="tpu_custom_call" | custom-call | tf_op jit(solution)/shard_map/pallas_call | solution.py:377
  146.5 2.1 %shard_map.42 = (f32[4096,128]{1,0:T(8,128)}, f32[4096,128]{1,0:T(8,128)}) custom-call(f32[4096,128]{1,0:T(8,128)S(1)} %get-tuple-element.6.re_ref, f32[4096,128]{1,0:T(8,128)S(1)} %get-tuple-element.7.im_ref), custom_call_target="tpu_custom_call" | custom-call | tf_op jit(solution)/shard_map/pallas_call | solution.py:406

commit v7 on v6

--- a/solution.py
+++ b/solution.py
@@ -275,12 +275,15 @@
                     ]
 
     buffers = (p0, p1, p2, p3)
+    nearest = (4 - z) % 4 + 2 * ((3 - z) // 3)
+    second = 1 + nearest % 2
+    toward = (nearest, second, 6 - nearest - second)
 
     def leave(j, stage):
         src, dst, sem = buffers[stage].at[j], buffers[stage + 1].at[j], last_sem.at[stage, j]
         axis = ORDERS[j][stage]
         if axis == "z":
-            for d in (2, 1, 3):
+            for d in toward:
                 to = (z + d) % 4
                 send(src.at[to], dst.at[z], 4 + stage, sem, device(to, y, x, c))
             dst[z] = src[z]
@@ -290,9 +293,11 @@
                 send(src.at[:, :, :, to], dst.at[:, :, :, y], 4 + stage, sem, device(z, to, x, c))
             dst[:, :, :, y] = src[:, :, :, y]
         else:
-            for d, t in ((2, 1), (2, 0), (1, 1), (3, 1), (1, 0), (3, 0), (0, 1)):
-                tx, tc = (x + d) % 4, (c + t) % 2
-                send(src.at[:, tc, tx], dst.at[:, c, x], 4 + stage, sem, device(z, y, tx, tc))
+            send(src.at[:, 1 - c, x], dst.at[:, c, x], 4 + stage, sem, device(z, y, x, 1 - c))
+            for tc in (1, 0):
+                for d in (2, 1, 3):
+                    tx = (x + d) % 4
+                    send(src.at[:, tc, tx], dst.at[:, c, x], 4 + stage, sem, device(z, y, tx, tc))
             dst[:, c, x] = src[:, c, x]
 
     def arrive(j, stage):

time: 149 us -> 149 us (level)
  no operation moved by 1% of the time
where the time goes in v7:
time: 149 us; the launch traced here: 148 us
  Pallas kernels  147 us (99%)
    pallas_call x1, Pallas kernels, body(): pl.pallas_call(kernel, out_shape=[pltpu.VMEM((4096, 128), F32)] * 2, in_s...  145 us

profile of v7, /device:TPU:1, one launch (start us, length us, event | category | flops | bytes accessed | tf_op | source)
XLA Modules:
  0.0 147.7 jit_solution(12701259517853043897)
XLA Ops:
  0.6 145.0 %shard_map.41 = (f32[4096,128]{1,0:T(8,128)S(1)}, f32[4096,128]{1,0:T(8,128)S(1)}) custom-call(f32[4,32,32,1,128]{4,3,2,1,0:T(1,128)} %bitcast.4, f32[4,32,32,1,128]{4,3,2,1,0:T(1,128)} %bitcast.5), custom_call_target="tpu_custom_call" | custom-call | tf_op jit(solution)/shard_map/pallas_call | solution.py:382
  145.6 2.1 %shard_map.42 = (f32[4096,128]{1,0:T(8,128)}, f32[4096,128]{1,0:T(8,128)}) custom-call(f32[4096,128]{1,0:T(8,128)S(1)} %get-tuple-element.6.re_ref, f32[4096,128]{1,0:T(8,128)S(1)} %get-tuple-element.7.im_ref), custom_call_target="tpu_custom_call" | custom-call | tf_op jit(solution)/shard_map/pallas_call | solution.py:411
